TPU v7x, 32 devices: a whole 2x2x4 slice. The times are simulated.
32 devices in a mesh: groups: 2 (over x), blk: 16 (over z, y, core).
Axes of the slice: x: 2, y: 2, z: 4, core: 2. Of those that a mesh axis runs over, the one named last changes fastest.
Arguments:
- walkers: bfloat16 [64, 65536], P(('groups', 'blk')), parts along dimension 0, may hold values from -6 to 6
- intersection_inv: bfloat16 [64, 4096], P(('groups', 'blk')), parts along dimension 0, may hold values from -0.75 to 0.75
- new_slot: int32 [64], P(('groups', 'blk')), parts along dimension 0, may hold values from 0 to 31, as said below
- cholesky: bfloat16 [2048, 64, 10240], P(('groups', 'blk')), parts along dimension 0, may hold values from -0.0234375 to 0.0234375
Outputs:
- moved_walkers: bfloat16 [64, 65536], P(('groups', 'blk')), parts along dimension 0
- moved_intersection_inv: bfloat16 [64, 4096], P(('groups', 'blk')), parts along dimension 0
- force_bias: float32 [64, 10240], P(('groups', 'blk')), parts along dimension 0
There are 2 independent parts, one for each index of `groups`. A program takes and returns all parts, laid end to end along the dimension named above; each array names one. Nothing has to cross between parts.
Inputs may be any that keep to these rules, and one draw needn't show every extreme that they name: new_slot is a permutation; the new owner of walker w is new_slot[w] // 2; the 2 walkers of one device go to 2 different owners, and new_slot[w] % 2 == w % 2.
All inputs are finite; a program needn't handle non-finite values.
Results may differ from a plain program's by a relative error of at most 0.0028.
Values may be sent and summed in bfloat16 or wider, within the bound.
No kernel may reach another device: no remote copies, remote signals or barrier semaphores. Data moves between devices by JAX's collectives and lax.ppermute only.
A program may use at most 128 MiB of HBM per device.

v0:
```python
import jax
import jax.numpy as jnp
from jax import lax
from jax.sharding import PartitionSpec as P


def local(walkers, intersection_inv, new_slot, cholesky):
    cycle_size = lax.axis_size("blk")
    my_index = lax.axis_index("blk")
    walk_dev = walkers.shape[0]
    walk_total = walk_dev * cycle_size
    orbit_local = cholesky.shape[0]
    occupied = cholesky.shape[1]
    chol_flat = cholesky.reshape(orbit_local * occupied, cholesky.shape[2])
    all_slots = lax.all_gather(new_slot, "blk", axis=0, tiled=True)
    anchor = (
        jnp.zeros((walk_total,), jnp.int32)
        .at[all_slots]
        .set(jnp.arange(walk_total, dtype=jnp.int32))
    )
    local_orbit = lax.all_to_all(walkers, "blk", split_axis=1, concat_axis=0, tiled=True)
    all_inverse = lax.all_gather(intersection_inv, "blk", axis=0, tiled=True)
    perm_orbit = local_orbit[anchor]
    perm_inverse = all_inverse[anchor]
    greens = jnp.einsum(
        "wpj,wij->wpi",
        perm_orbit.reshape(walk_total, orbit_local, occupied),
        perm_inverse.reshape(walk_total, occupied, occupied),
        preferred_element_type=jnp.float32,
    ).astype(jnp.bfloat16)
    green_orbit = greens.reshape(walk_total, orbit_local * occupied)
    moved_walk = lax.all_to_all(perm_orbit, "blk", split_axis=0, concat_axis=1, tiled=True)
    moved_inverse = lax.dynamic_slice_in_dim(perm_inverse, my_index * walk_dev, walk_dev, 0)
    force_bias = lax.psum_scatter(
        jnp.dot(green_orbit, chol_flat, preferred_element_type=jnp.float32),
        "blk",
        scatter_dimension=0,
        tiled=True,
    )
    return (moved_walk, moved_inverse, force_bias)


def solution(mesh):
    placed = (
        P(("groups", "blk"), None),
        P(("groups", "blk"), None),
        P(("groups", "blk")),
        P(("groups", "blk"), None, None),
    )
    return jax.shard_map(
        local,
        mesh=mesh,
        in_specs=placed,
        out_specs=(
            P(("groups", "blk"), None),
            P(("groups", "blk"), None),
            P(("groups", "blk"), None),
        ),
        check_vma=False,
    )
```

profile of v0, /device:TPU:0, one launch (start us, length us, event | category | flops | bytes accessed | tf_op | source)
XLA Modules:
  0.0 186.7 jit_solution(3166553028669388083)
XLA Ops:
  7.2 7.4 %all-to-all-start = ((bf16[2,16,4096]{2,0,1:T(2,128)(2,1)}), bf16[2,16,4096]{2,0,1:T(2,128)(2,1)S(1)}, u32[]{:S(2)}, u32[]{:S(2)}) async-start(bf16[2,16,4096]{2,0,1:T(2,128)(2,1)} %bitcast.16), calls=%async_computation | async-start | bytes 524288 | tf_op jit(solution)/shard_map/all_to_all | solution.py:21
  14.6 0.0 all-reduce.4.cloned.1.call-start
  14.7 1.3 fusion.2
  16.6 0.9 dynamic-update-slice
  17.5 12.4 %all-reduce = s32[32]{0:T(128)S(1)} all-reduce(s32[32]{0:T(128)S(1)} %dynamic-update-slice), channel_id=1, replica_groups=mesh['groups'=2,'blk'=16] {'blk'}, use_global_device_ids=true, to_apply=%add | all-reduce | flops 32 | bytes 256
  29.9 18.9 %all-gather = bf16[16,2,4096]{2,1,0:T(2,128)(2,1)S(1)} all-gather(bf16[1,2,4096]{2,1,0:T(2,128)(2,1)} %bitcast.17), channel_id=1, replica_groups=mesh['groups'=2,'blk'=16] {'blk'}, dimensions={0}, use_global_device_ids=true | all-gather | bytes 278528 | tf_op jit(solution)/shard_map/all_gather | solution.py:22
  48.8 0.1 reshape.53
  48.9 0.7 scatter_custom_fusion
  49.6 0.7 gather_fusion.1
  50.3 0.5 reshape.21
  50.9 0.0 all-to-all-done
  50.9 0.1 all_to_all.31
  51.0 0.7 gather_fusion
  51.7 0.5 reshape.20
  52.2 0.4 fusion.3
  52.6 30.0 %convolution_bitcast_fusion = f32[32,10240]{1,0:T(8,128)} fusion(bf16[64,64,10240]{2,1,0:T(8,128)(2,1)} %param.7, bf16[32,64,64]{2,1,0:T(8,128)(2,1)S(1)} %fusion.3), kind=kOutput, calls=%fused_computation.3 | convolution fusion | flops 2684354560 | bytes 85458944 | tf_op jit(solution)/shard_map/dot_general | solution.py:35
  82.7 0.0 all-reduce.4.cloned.1.call-update
  82.7 0.9 all_to_all.32
  83.6 3.5 %all-to-all-start.1 = ((bf16[16,2,4096]{2,1,0:T(2,128)(2,1)}), bf16[16,2,4096]{2,1,0:T(2,128)(2,1)S(1)}, u32[]{:S(2)}, u32[]{:S(2)}) async-start(bf16[16,2,4096]{2,1,0:T(2,128)(2,1)} %all_to_all.32), calls=%async_computation.1 | async-start | bytes 524288 | tf_op jit(solution)/shard_map/all_to_all | solution.py:32
  87.8 0.6 constant_dynamic-slice_fusion.1
  88.4 10.8 %all-to-all-done.1 = bf16[16,2,4096]{2,1,0:T(2,128)(2,1)S(1)} async-done(((bf16[16,2,4096]{2,1,0:T(2,128)(2,1)}), bf16[16,2,4096]{2,1,0:T(2,128)(2,1)S(1)}, u32[]{:S(2)}, u32[]{:S(2)}) %all-to-all-start.1) | async-done | bytes 262176 | tf_op jit(solution)/shard_map/all_to_all | solution.py:32
  99.2 78.3 %all-reduce.4.cloned.1.call-done = f32[32,10240]{1,0:T(8,128)} async-done(((f32[32,10240]{1,0:T(8,128)}), f32[32,10240]{1,0:T(8,128)}) %all-reduce.4.cloned.1.call-update) | async-done | bytes 1310736
  177.5 1.6 constant_dynamic-slice_fusion
  179.2 0.7 copy.17
  (5 shorter events, 0.0 us)
Async XLA Ops:
  7.2 43.7 %all-to-all-start = ((bf16[2,16,4096]{2,0,1:T(2,128)(2,1)}), bf16[2,16,4096]{2,0,1:T(2,128)(2,1)S(1)}, u32[]{:S(2)}, u32[]{:S(2)}) async-start(bf16[2,16,4096]{2,0,1:T(2,128)(2,1)} %bitcast.16), calls=%async_computation | async-start | bytes 524288 | tf_op jit(solution)/shard_map/all_to_all | solution.py:21
  14.6 162.9 %all-reduce.4.cloned.1.call-start = ((), (), s32[]{:S(2)}) async-start(), calls=%async_computation.2 | async-start | bytes 2621440
  83.6 15.7 %all-to-all-start.1 = ((bf16[16,2,4096]{2,1,0:T(2,128)(2,1)}), bf16[16,2,4096]{2,1,0:T(2,128)(2,1)S(1)}, u32[]{:S(2)}, u32[]{:S(2)}) async-start(bf16[16,2,4096]{2,1,0:T(2,128)(2,1)} %all_to_all.32), calls=%async_computation.1 | async-start | bytes 524288 | tf_op jit(solution)/shard_map/all_to_all | solution.py:32
Sparse Core Ops, SparseCore 0:
  82.8 94.7 all-reduce.3
where the time goes:
time: 187 us
  waiting for transfers between devices  89.2 us (48%)
  blocking collectives  31.3 us (17%)
  matrix products  30.4 us (16%)
  between operations  15.5 us (8%)
  starting transfers between devices  11 us (6%)
  local copies, waits for them, and re-layouts  9.4 us (5%)
    unnamed x2, waiting for transfers between devices  78.3 us
    dot_general x1, matrix products, local(): jnp.dot(green_orbit, chol_flat, preferred_element_type=jnp.float32)  30 us
    all_gather x1, blocking collectives, local(): all_inverse = lax.all_gather(intersection_inv, 'blk', axis=0, tiled=True)  18.9 us
    unnamed x1, blocking collectives  12.4 us
    all_to_all x1, waiting for transfers between devices, local(): lax.all_to_all(perm_orbit, 'blk', split_axis=0, concat_axis=1, tiled=True)  10.8 us
    all_to_all x1, starting transfers between devices, local(): lax.all_to_all(walkers, 'blk', split_axis=1, concat_axis=0, tiled=True)  7.43 us
    unnamed x5, local copies, waits for them, and re-layouts  4.62 us
  transfers between devices with their start and end apart: 3, of which 2 were waited for; matrix products, arithmetic and copies ran while one was open for 3% of the time, Pallas kernels for 0%

commit v1 on v0

--- a/solution.py
+++ b/solution.py
@@ -19,7 +19,12 @@
         .set(jnp.arange(walk_total, dtype=jnp.int32))
     )
     local_orbit = lax.all_to_all(walkers, "blk", split_axis=1, concat_axis=0, tiled=True)
-    all_inverse = lax.all_gather(intersection_inv, "blk", axis=0, tiled=True)
+    ring = [intersection_inv]
+    for hop in range(15):
+        ring.append(lax.ppermute(ring[-1], "blk", [(dev, (dev + 1) % 16) for dev in range(16)]))
+    all_inverse = jnp.roll(
+        jnp.concatenate(ring[::-1], axis=0), (lax.axis_index("blk") + 1) * ring[0].shape[0], axis=0
+    )
     perm_orbit = local_orbit[anchor]
     perm_inverse = all_inverse[anchor]
     greens = jnp.einsum(

time: 187 us -> 252 us (1.35)
  waiting for transfers between devices: 89.2 us -> 172 us
  blocking collectives: 31.3 us -> 12.4 us
    ppermute x0 -> x15, waiting for transfers between devices: none -> 82 us  [local(): lax.ppermute(ring[-1], 'blk', [(dev, (dev + 1) % 16) for dev in range(16)])]
    all_gather x1 -> x0, blocking collectives: 18.9 us -> none  [local(): all_inverse = lax.all_gather(intersection_inv, 'blk', axis=0, tiled=True)]
  transfers between devices with their start and end apart: 3 -> 18, of which waited for: 2 -> 16; matrix products, arithmetic and copies ran while one was open for 3% -> 3% of each run, Pallas kernels for 0% -> 0%
where the time goes in v1:
time: 252 us; the launch traced here: 251 us
  waiting for transfers between devices  172 us (68%)
  matrix products  30.4 us (12%)
  between operations  15.5 us (6%)
  blocking collectives  12.4 us (5%)
  local copies, waits for them, and re-layouts  11.6 us (5%)
  starting transfers between devices  9.98 us (4%)
    ppermute x15, waiting for transfers between devices, local(): lax.ppermute(ring[-1], 'blk', [(dev, (dev + 1) % 16) for dev in range(16)])  82 us
    unnamed x2, waiting for transfers between devices  78.9 us
    dot_general x1, matrix products, local(): jnp.dot(green_orbit, chol_flat, preferred_element_type=jnp.float32)  30 us
    unnamed x1, blocking collectives  12.4 us
    all_to_all x1, waiting for transfers between devices, local(): lax.all_to_all(perm_orbit, 'blk', split_axis=0, concat_axis=1, tiled=True)  10.6 us
    all_to_all x1, starting transfers between devices, local(): lax.all_to_all(walkers, 'blk', split_axis=1, concat_axis=0, tiled=True)  5.82 us
  transfers between devices with their start and end apart: 18, of which 16 were waited for; matrix products, arithmetic and copies ran while one was open for 3% of the time, Pallas kernels for 0%

profile of v1, /device:TPU:0, one launch (start us, length us, event | category | flops | bytes accessed | tf_op | source)
XLA Modules:
  0.0 251.5 jit_solution(16933391909163059842)
XLA Ops:
  7.2 0.5 collective-permute-start
  7.7 6.6 %collective-permute-done = bf16[2,4096]{1,0:T(2,128)(2,1)S(1)} collective-permute-done((bf16[2,4096]{1,0:T(2,128)(2,1)}, bf16[2,4096]{1,0:T(2,128)(2,1)S(1)}, u32[]{:S(2)}, u32[]{:S(2)}) %collective-permute-start) | collective-permute-done | bytes 16416 | tf_op jit(solution)/shard_map/ppermute | solution.py:24
  14.3 0.0 collective-permute-start.1
  14.3 5.9 %collective-permute-done.1 = bf16[2,4096]{1,0:T(2,128)(2,1)S(1)} collective-permute-done((bf16[2,4096]{1,0:T(2,128)(2,1)S(1)}, bf16[2,4096]{1,0:T(2,128)(2,1)S(1)}, u32[]{:S(2)}, u32[]{:S(2)}) %collective-permute-start.1) | collective-permute-done | bytes 16416 | tf_op jit(solution)/shard_map/ppermute | solution.py:24
  20.2 0.0 collective-permute-start.2
  20.2 5.9 %collective-permute-done.2 = bf16[2,4096]{1,0:T(2,128)(2,1)S(1)} collective-permute-done((bf16[2,4096]{1,0:T(2,128)(2,1)S(1)}, bf16[2,4096]{1,0:T(2,128)(2,1)S(1)}, u32[]{:S(2)}, u32[]{:S(2)}) %collective-permute-start.2) | collective-permute-done | bytes 16416 | tf_op jit(solution)/shard_map/ppermute | solution.py:24
  26.0 0.0 collective-permute-start.3
  26.1 5.9 %collective-permute-done.3 = bf16[2,4096]{1,0:T(2,128)(2,1)S(1)} collective-permute-done((bf16[2,4096]{1,0:T(2,128)(2,1)S(1)}, bf16[2,4096]{1,0:T(2,128)(2,1)S(1)}, u32[]{:S(2)}, u32[]{:S(2)}) %collective-permute-start.3) | collective-permute-done | bytes 16416 | tf_op jit(solution)/shard_map/ppermute | solution.py:24
  31.9 0.0 collective-permute-start.4
  31.9 5.9 %collective-permute-done.4 = bf16[2,4096]{1,0:T(2,128)(2,1)S(1)} collective-permute-done((bf16[2,4096]{1,0:T(2,128)(2,1)S(1)}, bf16[2,4096]{1,0:T(2,128)(2,1)S(1)}, u32[]{:S(2)}, u32[]{:S(2)}) %collective-permute-start.4) | collective-permute-done | bytes 16416 | tf_op jit(solution)/shard_map/ppermute | solution.py:24
  37.8 0.0 collective-permute-start.5
  37.8 5.9 %collective-permute-done.5 = bf16[2,4096]{1,0:T(2,128)(2,1)S(1)} collective-permute-done((bf16[2,4096]{1,0:T(2,128)(2,1)S(1)}, bf16[2,4096]{1,0:T(2,128)(2,1)S(1)}, u32[]{:S(2)}, u32[]{:S(2)}) %collective-permute-start.5) | collective-permute-done | bytes 16416 | tf_op jit(solution)/shard_map/ppermute | solution.py:24
  43.6 0.0 collective-permute-start.6
  43.6 5.9 %collective-permute-done.6 = bf16[2,4096]{1,0:T(2,128)(2,1)S(1)} collective-permute-done((bf16[2,4096]{1,0:T(2,128)(2,1)S(1)}, bf16[2,4096]{1,0:T(2,128)(2,1)S(1)}, u32[]{:S(2)}, u32[]{:S(2)}) %collective-permute-start.6) | collective-permute-done | bytes 16416 | tf_op jit(solution)/shard_map/ppermute | solution.py:24
  49.5 0.0 collective-permute-start.7
  49.5 5.9 %collective-permute-done.7 = bf16[2,4096]{1,0:T(2,128)(2,1)S(1)} collective-permute-done((bf16[2,4096]{1,0:T(2,128)(2,1)S(1)}, bf16[2,4096]{1,0:T(2,128)(2,1)S(1)}, u32[]{:S(2)}, u32[]{:S(2)}) %collective-permute-start.7) | collective-permute-done | bytes 16416 | tf_op jit(solution)/shard_map/ppermute | solution.py:24
  55.4 0.0 collective-permute-start.8
  55.4 5.9 %collective-permute-done.8 = bf16[2,4096]{1,0:T(2,128)(2,1)S(1)} collective-permute-done((bf16[2,4096]{1,0:T(2,128)(2,1)S(1)}, bf16[2,4096]{1,0:T(2,128)(2,1)S(1)}, u32[]{:S(2)}, u32[]{:S(2)}) %collective-permute-start.8) | collective-permute-done | bytes 16416 | tf_op jit(solution)/shard_map/ppermute | solution.py:24
  61.2 0.0 collective-permute-start.9
  61.2 5.9 %collective-permute-done.9 = bf16[2,4096]{1,0:T(2,128)(2,1)S(1)} collective-permute-done((bf16[2,4096]{1,0:T(2,128)(2,1)S(1)}, bf16[2,4096]{1,0:T(2,128)(2,1)S(1)}, u32[]{:S(2)}, u32[]{:S(2)}) %collective-permute-start.9) | collective-permute-done | bytes 16416 | tf_op jit(solution)/shard_map/ppermute | solution.py:24
  67.1 0.0 collective-permute-start.10
  67.1 5.9 %collective-permute-done.10 = bf16[2,4096]{1,0:T(2,128)(2,1)S(1)} collective-permute-done((bf16[2,4096]{1,0:T(2,128)(2,1)S(1)}, bf16[2,4096]{1,0:T(2,128)(2,1)S(1)}, u32[]{:S(2)}, u32[]{:S(2)}) %collective-permute-start.10) | collective-permute-done | bytes 16416 | tf_op jit(solution)/shard_map/ppermute | solution.py:24
  72.9 0.0 collective-permute-start.11
  72.9 5.8 %all-to-all-start = ((bf16[2,16,4096]{2,0,1:T(2,128)(2,1)}), bf16[2,16,4096]{2,0,1:T(2,128)(2,1)S(1)}, u32[]{:S(2)}, u32[]{:S(2)}) async-start(bf16[2,16,4096]{2,0,1:T(2,128)(2,1)} %bitcast.15), calls=%async_computation | async-start | bytes 524288 | tf_op jit(solution)/shard_map/all_to_all | solution.py:21
  78.8 0.0 all-reduce.4.cloned.1.call-start
  78.8 1.3 fusion.2
  80.8 0.9 dynamic-update-slice
  81.7 12.4 %all-reduce = s32[32]{0:T(128)S(1)} all-reduce(s32[32]{0:T(128)S(1)} %dynamic-update-slice), channel_id=1, replica_groups=mesh['groups'=2,'blk'=16] {'blk'}, use_global_device_ids=true, to_apply=%add | all-reduce | flops 32 | bytes 256
  94.1 0.0 collective-permute-done.11
  94.1 0.0 collective-permute-start.12
  94.1 0.7 scatter_custom_fusion
  94.8 5.2 %collective-permute-done.12 = bf16[2,4096]{1,0:T(2,128)(2,1)S(1)} collective-permute-done((bf16[2,4096]{1,0:T(2,128)(2,1)S(1)}, bf16[2,4096]{1,0:T(2,128)(2,1)S(1)}, u32[]{:S(2)}, u32[]{:S(2)}) %collective-permute-start.12) | collective-permute-done | bytes 16416 | tf_op jit(solution)/shard_map/ppermute | solution.py:24
  100.0 0.0 collective-permute-start.13
  100.0 5.9 %collective-permute-done.13 = bf16[2,4096]{1,0:T(2,128)(2,1)S(1)} collective-permute-done((bf16[2,4096]{1,0:T(2,128)(2,1)S(1)}, bf16[2,4096]{1,0:T(2,128)(2,1)S(1)}, u32[]{:S(2)}, u32[]{:S(2)}) %collective-permute-start.13) | collective-permute-done | bytes 16416 | tf_op jit(solution)/shard_map/ppermute | solution.py:24
  105.8 0.0 collective-permute-start.14
  105.9 5.8 %collective-permute-done.14 = bf16[2,4096]{1,0:T(2,128)(2,1)S(1)} collective-permute-done((bf16[2,4096]{1,0:T(2,128)(2,1)S(1)}, bf16[2,4096]{1,0:T(2,128)(2,1)S(1)}, u32[]{:S(2)}, u32[]{:S(2)}) %collective-permute-start.14) | collective-permute-done | bytes 16416 | tf_op jit(solution)/shard_map/ppermute | solution.py:24
  111.7 2.3 concatenate.6
  114.0 0.1 constant_dynamic-slice_fusion.2
  114.1 0.7 gather_fusion.1
  114.8 0.5 reshape.21
  115.3 0.0 all-to-all-done
  115.3 0.1 all_to_all.31
  115.4 0.7 gather_fusion
  116.1 0.5 reshape.20
  116.7 0.4 fusion.3
  117.1 30.0 %convolution_bitcast_fusion = f32[32,10240]{1,0:T(8,128)} fusion(bf16[64,64,10240]{2,1,0:T(8,128)(2,1)} %param.7, bf16[32,64,64]{2,1,0:T(8,128)(2,1)S(1)} %fusion.3), kind=kOutput, calls=%fused_computation.3 | convolution fusion | flops 2684354560 | bytes 85458944 | tf_op jit(solution)/shard_map/dot_general | solution.py:40
  147.1 0.0 all-reduce.4.cloned.1.call-update
  147.1 0.9 all_to_all.32
  148.0 3.5 %all-to-all-start.1 = ((bf16[16,2,4096]{2,1,0:T(2,128)(2,1)}), bf16[16,2,4096]{2,1,0:T(2,128)(2,1)S(1)}, u32[]{:S(2)}, u32[]{:S(2)}) async-start(bf16[16,2,4096]{2,1,0:T(2,128)(2,1)} %all_to_all.32), calls=%async_computation.1 | async-start | bytes 524288 | tf_op jit(solution)/shard_map/all_to_all | solution.py:37
  152.2 0.6 constant_dynamic-slice_fusion.1
  152.8 10.6 %all-to-all-done.1 = bf16[16,2,4096]{2,1,0:T(2,128)(2,1)S(1)} async-done(((bf16[16,2,4096]{2,1,0:T(2,128)(2,1)}), bf16[16,2,4096]{2,1,0:T(2,128)(2,1)S(1)}, u32[]{:S(2)}, u32[]{:S(2)}) %all-to-all-start.1) | async-done | bytes 262176 | tf_op jit(solution)/shard_map/all_to_all | solution.py:37
  163.4 78.9 %all-reduce.4.cloned.1.call-done = f32[32,10240]{1,0:T(8,128)} async-done(((f32[32,10240]{1,0:T(8,128)}), f32[32,10240]{1,0:T(8,128)}) %all-reduce.4.cloned.1.call-update) | async-done | bytes 1310736
  242.3 1.6 constant_dynamic-slice_fusion
  243.9 0.7 copy.17
  (5 shorter events, 0.0 us)
Async XLA Ops:
  7.2 7.2 %collective-permute-start = (bf16[2,4096]{1,0:T(2,128)(2,1)}, bf16[2,4096]{1,0:T(2,128)(2,1)S(1)}, u32[]{:S(2)}, u32[]{:S(2)}) collective-permute-start(bf16[2,4096]{1,0:T(2,128)(2,1)} %param.5), channel_id=1, source_target_pairs={{0,1},{1,2},{2,3},{3,4},{4,5},{5,6},{6,7},{7,8},{8,9},{9,10},{10,1... | collective-permute-start | bytes 49160 | tf_op jit(solution)/shard_map/ppermute | solution.py:24
  14.3 5.9 %collective-permute-start.1 = (bf16[2,4096]{1,0:T(2,128)(2,1)S(1)}, bf16[2,4096]{1,0:T(2,128)(2,1)S(1)}, u32[]{:S(2)}, u32[]{:S(2)}) collective-permute-start(bf16[2,4096]{1,0:T(2,128)(2,1)S(1)} %collective-permute-done), channel_id=1, source_target_pairs={{0,1},{1,2},{2,3},{3,4},{4,5},{5,6},{6,7},{7,8},{8,9},{9,10},{10,1... | collective-permute-start | bytes 49160 | tf_op jit(solution)/shard_map/ppermute | solution.py:24
  20.2 5.9 %collective-permute-start.2 = (bf16[2,4096]{1,0:T(2,128)(2,1)S(1)}, bf16[2,4096]{1,0:T(2,128)(2,1)S(1)}, u32[]{:S(2)}, u32[]{:S(2)}) collective-permute-start(bf16[2,4096]{1,0:T(2,128)(2,1)S(1)} %collective-permute-done.1), channel_id=1, source_target_pairs={{0,1},{1,2},{2,3},{3,4},{4,5},{5,6},{6,7},{7,8},{8,9},{9,10},{10,1... | collective-permute-start | bytes 49160 | tf_op jit(solution)/shard_map/ppermute | solution.py:24
  26.0 5.9 %collective-permute-start.3 = (bf16[2,4096]{1,0:T(2,128)(2,1)S(1)}, bf16[2,4096]{1,0:T(2,128)(2,1)S(1)}, u32[]{:S(2)}, u32[]{:S(2)}) collective-permute-start(bf16[2,4096]{1,0:T(2,128)(2,1)S(1)} %collective-permute-done.2), channel_id=1, source_target_pairs={{0,1},{1,2},{2,3},{3,4},{4,5},{5,6},{6,7},{7,8},{8,9},{9,10},{10,1... | collective-permute-start | bytes 49160 | tf_op jit(solution)/shard_map/ppermute | solution.py:24
  31.9 5.9 %collective-permute-start.4 = (bf16[2,4096]{1,0:T(2,128)(2,1)S(1)}, bf16[2,4096]{1,0:T(2,128)(2,1)S(1)}, u32[]{:S(2)}, u32[]{:S(2)}) collective-permute-start(bf16[2,4096]{1,0:T(2,128)(2,1)S(1)} %collective-permute-done.3), channel_id=1, source_target_pairs={{0,1},{1,2},{2,3},{3,4},{4,5},{5,6},{6,7},{7,8},{8,9},{9,10},{10,1... | collective-permute-start | bytes 49160 | tf_op jit(solution)/shard_map/ppermute | solution.py:24
  37.8 5.9 %collective-permute-start.5 = (bf16[2,4096]{1,0:T(2,128)(2,1)S(1)}, bf16[2,4096]{1,0:T(2,128)(2,1)S(1)}, u32[]{:S(2)}, u32[]{:S(2)}) collective-permute-start(bf16[2,4096]{1,0:T(2,128)(2,1)S(1)} %collective-permute-done.4), channel_id=1, source_target_pairs={{0,1},{1,2},{2,3},{3,4},{4,5},{5,6},{6,7},{7,8},{8,9},{9,10},{10,1... | collective-permute-start | bytes 49160 | tf_op jit(solution)/shard_map/ppermute | solution.py:24
  43.6 5.9 %collective-permute-start.6 = (bf16[2,4096]{1,0:T(2,128)(2,1)S(1)}, bf16[2,4096]{1,0:T(2,128)(2,1)S(1)}, u32[]{:S(2)}, u32[]{:S(2)}) collective-permute-start(bf16[2,4096]{1,0:T(2,128)(2,1)S(1)} %collective-permute-done.5), channel_id=1, source_target_pairs={{0,1},{1,2},{2,3},{3,4},{4,5},{5,6},{6,7},{7,8},{8,9},{9,10},{10,1... | collective-permute-start | bytes 49160 | tf_op jit(solution)/shard_map/ppermute | solution.py:24
  49.5 5.9 %collective-permute-start.7 = (bf16[2,4096]{1,0:T(2,128)(2,1)S(1)}, bf16[2,4096]{1,0:T(2,128)(2,1)S(1)}, u32[]{:S(2)}, u32[]{:S(2)}) collective-permute-start(bf16[2,4096]{1,0:T(2,128)(2,1)S(1)} %collective-permute-done.6), channel_id=1, source_target_pairs={{0,1},{1,2},{2,3},{3,4},{4,5},{5,6},{6,7},{7,8},{8,9},{9,10},{10,1... | collective-permute-start | bytes 49160 | tf_op jit(solution)/shard_map/ppermute | solution.py:24
  55.4 5.9 %collective-permute-start.8 = (bf16[2,4096]{1,0:T(2,128)(2,1)S(1)}, bf16[2,4096]{1,0:T(2,128)(2,1)S(1)}, u32[]{:S(2)}, u32[]{:S(2)}) collective-permute-start(bf16[2,4096]{1,0:T(2,128)(2,1)S(1)} %collective-permute-done.7), channel_id=1, source_target_pairs={{0,1},{1,2},{2,3},{3,4},{4,5},{5,6},{6,7},{7,8},{8,9},{9,10},{10,1... | collective-permute-start | bytes 49160 | tf_op jit(solution)/shard_map/ppermute | solution.py:24
  61.2 5.9 %collective-permute-start.9 = (bf16[2,4096]{1,0:T(2,128)(2,1)S(1)}, bf16[2,4096]{1,0:T(2,128)(2,1)S(1)}, u32[]{:S(2)}, u32[]{:S(2)}) collective-permute-start(bf16[2,4096]{1,0:T(2,128)(2,1)S(1)} %collective-permute-done.8), channel_id=1, source_target_pairs={{0,1},{1,2},{2,3},{3,4},{4,5},{5,6},{6,7},{7,8},{8,9},{9,10},{10,1... | collective-permute-start | bytes 49160 | tf_op jit(solution)/shard_map/ppermute | solution.py:24
  67.1 5.9 %collective-permute-start.10 = (bf16[2,4096]{1,0:T(2,128)(2,1)S(1)}, bf16[2,4096]{1,0:T(2,128)(2,1)S(1)}, u32[]{:S(2)}, u32[]{:S(2)}) collective-permute-start(bf16[2,4096]{1,0:T(2,128)(2,1)S(1)} %collective-permute-done.9), channel_id=1, source_target_pairs={{0,1},{1,2},{2,3},{3,4},{4,5},{5,6},{6,7},{7,8},{8,9},{9,10},{10,1... | collective-permute-start | bytes 49160 | tf_op jit(solution)/shard_map/ppermute | solution.py:24
  72.9 21.2 %collective-permute-start.11 = (bf16[2,4096]{1,0:T(2,128)(2,1)S(1)}, bf16[2,4096]{1,0:T(2,128)(2,1)S(1)}, u32[]{:S(2)}, u32[]{:S(2)}) collective-permute-start(bf16[2,4096]{1,0:T(2,128)(2,1)S(1)} %collective-permute-done.10), channel_id=1, source_target_pairs={{0,1},{1,2},{2,3},{3,4},{4,5},{5,6},{6,7},{7,8},{8,9},{9,10},{10,1... | collective-permute-start | bytes 49160 | tf_op jit(solution)/shard_map/ppermute | solution.py:24
  72.9 42.4 %all-to-all-start = ((bf16[2,16,4096]{2,0,1:T(2,128)(2,1)}), bf16[2,16,4096]{2,0,1:T(2,128)(2,1)S(1)}, u32[]{:S(2)}, u32[]{:S(2)}) async-start(bf16[2,16,4096]{2,0,1:T(2,128)(2,1)} %bitcast.15), calls=%async_computation | async-start | bytes 524288 | tf_op jit(solution)/shard_map/all_to_all | solution.py:21
  78.8 163.5 %all-reduce.4.cloned.1.call-start = ((), (), s32[]{:S(2)}) async-start(), calls=%async_computation.2 | async-start | bytes 2621440
  94.1 5.9 %collective-permute-start.12 = (bf16[2,4096]{1,0:T(2,128)(2,1)S(1)}, bf16[2,4096]{1,0:T(2,128)(2,1)S(1)}, u32[]{:S(2)}, u32[]{:S(2)}) collective-permute-start(bf16[2,4096]{1,0:T(2,128)(2,1)S(1)} %collective-permute-done.11), channel_id=1, source_target_pairs={{0,1},{1,2},{2,3},{3,4},{4,5},{5,6},{6,7},{7,8},{8,9},{9,10},{10,1... | collective-permute-start | bytes 49160 | tf_op jit(solution)/shard_map/ppermute | solution.py:24
  100.0 5.9 %collective-permute-start.13 = (bf16[2,4096]{1,0:T(2,128)(2,1)S(1)}, bf16[2,4096]{1,0:T(2,128)(2,1)S(1)}, u32[]{:S(2)}, u32[]{:S(2)}) collective-permute-start(bf16[2,4096]{1,0:T(2,128)(2,1)S(1)} %collective-permute-done.12), channel_id=1, source_target_pairs={{0,1},{1,2},{2,3},{3,4},{4,5},{5,6},{6,7},{7,8},{8,9},{9,10},{10,1... | collective-permute-start | bytes 49160 | tf_op jit(solution)/shard_map/ppermute | solution.py:24
  105.8 5.9 %collective-permute-start.14 = (bf16[2,4096]{1,0:T(2,128)(2,1)S(1)}, bf16[2,4096]{1,0:T(2,128)(2,1)S(1)}, u32[]{:S(2)}, u32[]{:S(2)}) collective-permute-start(bf16[2,4096]{1,0:T(2,128)(2,1)S(1)} %collective-permute-done.13), channel_id=1, source_target_pairs={{0,1},{1,2},{2,3},{3,4},{4,5},{5,6},{6,7},{7,8},{8,9},{9,10},{10,1... | collective-permute-start | bytes 49160 | tf_op jit(solution)/shard_map/ppermute | solution.py:24
  148.0 15.4 %all-to-all-start.1 = ((bf16[16,2,4096]{2,1,0:T(2,128)(2,1)}), bf16[16,2,4096]{2,1,0:T(2,128)(2,1)S(1)}, u32[]{:S(2)}, u32[]{:S(2)}) async-start(bf16[16,2,4096]{2,1,0:T(2,128)(2,1)} %all_to_all.32), calls=%async_computation.1 | async-start | bytes 524288 | tf_op jit(solution)/shard_map/all_to_all | solution.py:37
Sparse Core Ops, SparseCore 0:
  147.2 95.0 all-reduce.3
